TPU v7x, 64 devices: a 2x2x8 block of a 4x4x8 slice. The times are simulated.
64 devices in a mesh: dp: 8 (over x, y, core), tp: 8 (over z).
Axes of the slice: x: 2, y: 2, z: 8, core: 2. Of those that a mesh axis runs over, the one named last changes fastest.
The devices are a block of a 4x4x8 slice.
Arguments:
- x: bfloat16 [1024, 7168], P('dp'), parts along dimension 0
- w_gate: bfloat16 [7168, 18432], P(None, 'tp')
- w_up: bfloat16 [7168, 18432], P(None, 'tp')
- w_down: bfloat16 [18432, 7168], P('tp')
Outputs:
- output: bfloat16 [1024, 7168], P('dp'), parts along dimension 0
There are 8 independent parts. A program takes and returns all parts, laid end to end along the dimension named above; an argument that names none is the same for every part.
All inputs are finite; a program needn't handle non-finite values.
Results may differ from a plain program's by a relative error of at most 0.016.
Values are sent between devices in bfloat16 or wider.
A program may use at most 768 MiB of HBM per device.

v0:
```python
import jax
import jax.numpy as jnp
from jax import lax
from jax.sharding import PartitionSpec as P


def solution(mesh):
    def step(x, w_gate, w_up, w_down):
        gate = jnp.dot(x, w_gate, preferred_element_type=jnp.float32)
        up = jnp.dot(x, w_up, preferred_element_type=jnp.float32)
        hidden = (jax.nn.silu(gate) * up).astype(jnp.bfloat16)
        term = jnp.dot(hidden, w_down, preferred_element_type=jnp.float32).astype(jnp.bfloat16)
        return lax.psum(term, "tp")

    return jax.shard_map(
        step,
        mesh=mesh,
        in_specs=(P("dp", None), P(None, "tp"), P(None, "tp"), P("tp", None)),
        out_specs=P("dp", None),
        check_vma=False,
    )
```

profile of v0, /device:TPU:30, one launch (start us, length us, event | category | flops | bytes accessed | tf_op | source)
XLA Modules:
  0.0 133.4 jit_solution(17820568864797267531)
XLA Ops:
  6.5 0.0 copy-start
  6.6 0.0 all-reduce.2.cloned.1.call-start
  6.6 1.5 %copy-done = bf16[128,7168]{1,0:T(8,128)(2,1)S(1)} copy-done((bf16[128,7168]{1,0:T(8,128)(2,1)S(1)}, bf16[128,7168]{1,0:T(8,128)(2,1)}, u32[]{:S(2)}) %copy-start) | copy-done | bytes 1835032
  8.1 13.0 %fusion.2 = f32[128,2304]{1,0:T(8,128)S(1)} fusion(bf16[128,7168]{1,0:T(8,128)(2,1)S(1)} %copy-done, bf16[7168,2304]{1,0:T(8,128)(2,1)} %param.5), kind=kOutput, calls=%fused_computation.4 | convolution fusion | flops 4227858432 | bytes 36044800 | tf_op jit(solution)/shard_map/dot_general | solution.py:9
  21.0 25.6 %convolution_convert_fusion = bf16[128,7168]{1,0:T(8,128)(2,1)} fusion(bf16[2304,7168]{1,0:T(8,128)(2,1)} %param.7, bf16[128,7168]{1,0:T(8,128)(2,1)S(1)} %copy-done, bf16[7168,2304]{1,0:T(8,128)(2,1)} %param.6, f32[128,2304]{1,0:T(8,128)S(1)} %fusion.2), kind=kOutput, calls=%fused_computation | convolution fusion | flops 8458403840 | bytes 70909952 | tf_op jit(solution)/shard_map/dot_general | solution.py:12
  46.6 0.1 all-reduce.2.cloned.1.call-update
  46.7 0.0 copy-start.1
  46.7 77.0 %all-reduce.2.cloned.1.call-done = bf16[128,7168]{1,0:T(8,128)(2,1)} async-done(((bf16[128,7168]{1,0:T(8,128)(2,1)}), bf16[128,7168]{1,0:T(8,128)(2,1)}) %all-reduce.2.cloned.1.call-update) | async-done | bytes 1835024 | tf_op jit(solution)/shard_map/psum | solution.py:13
  123.7 2.8 %copy.6 = bf16[128,7168]{1,0:T(8,128)(2,1)} copy(bf16[128,7168]{1,0:T(8,128)(2,1)} %all-reduce.2.cloned.1.call-done) | data formatting | bytes 3670016
  126.5 0.0 copy-done.1
Async XLA Ops:
  6.5 1.5 %copy-start = (bf16[128,7168]{1,0:T(8,128)(2,1)S(1)}, bf16[128,7168]{1,0:T(8,128)(2,1)}, u32[]{:S(2)}) copy-start(bf16[128,7168]{1,0:T(8,128)(2,1)} %param.4) | copy-start | bytes 5505028
  6.6 117.2 %all-reduce.2.cloned.1.call-start = ((), (), s32[]{:S(2)}) async-start(), calls=%async_computation | async-start | bytes 3670016 | tf_op jit(solution)/shard_map/psum | solution.py:13
  46.7 79.9 %copy-start.1 = (bf16[128,7168]{1,0:T(8,128)(2,1)S(1)}, bf16[128,7168]{1,0:T(8,128)(2,1)}, u32[]{:S(2)}) copy-start(bf16[128,7168]{1,0:T(8,128)(2,1)} %param.4) | copy-start | bytes 5505028
Sparse Core Ops, SparseCore 0:
  46.8 76.8 all-reduce.1
where the time goes:
time: 134 us; the launch traced here: 133 us
  waiting for transfers between devices  77 us (57%)
  matrix products  38.6 us (29%)
  between operations  13.4 us (10%)
  local copies, waits for them, and re-layouts  4.35 us (3%)
    psum x1, waiting for transfers between devices, step(): return lax.psum(term, 'tp')  77 us
    dot_general x1, matrix products, step(): jnp.dot(hidden, w_down, preferred_element_type=jnp.float32)  25.6 us
    dot_general x1, matrix products, step(): gate = jnp.dot(x, w_gate, preferred_element_type=jnp.float32)  13 us
    unnamed x5, local copies, waits for them, and re-layouts  4.35 us
  transfers between devices with their start and end apart: 1, of which 1 were waited for; matrix products, arithmetic and copies ran while one was open for 0% of the time, Pallas kernels for 0%

commit v1 on v0

v1 whole, which is shorter than its diff:
```python
import functools

import jax
import jax.numpy as jnp
from jax import lax
from jax.experimental import pallas as pl
from jax.experimental.pallas import tpu as pltpu
from jax.sharding import PartitionSpec as P

F32, BF16 = jnp.float32, jnp.bfloat16
CHUNK = 512
SLOTS = 8
GROUPS = (1, 1, 2, 2, 2, 2, 2, 1, 1)
SUBS = 4


def kernel(n, x_hbm, wg_hbm, wu_hbm, wd_hbm, y_hbm, xbuf, wgu, wd, acc, hid, term, psend, precv, rsend, rrecv, y,
           x_sem, xs_sem, xr_sem, w_sem, d_sem, ps_sem, pr_sem, s_sem, r_sem, o_sem):
    rows, depth = x_hbm.shape
    share = wg_hbm.shape[1]
    part = share // 2
    cols = depth // n
    half_rows = rows // 2
    sub_rows = half_rows // SUBS
    far = n // 2
    chunks = depth // CHUNK

    dp, me = lax.axis_index("dp"), lax.axis_index("tp")
    side = lax.rem(dp, 2)
    partner = {"dp": dp + 1 - 2 * side}
    right, left = {"tp": lax.rem(me + 1, n)}, {"tp": lax.rem(me + n - 1, n)}
    to = (right, left)
    mesh_id = pl.DeviceIdType.MESH

    barrier = pltpu.get_barrier_semaphore()
    for other in (left, right, partner):
        pl.semaphore_signal(barrier, inc=1, device_id=other, device_id_type=mesh_id)

    def owner(off):
        return lax.rem(me + off + n, n)

    mine = pl.ds(pl.multiple_of(side * part, 128), part)

    def x_copy(k):
        span = pl.ds(k * CHUNK, CHUNK)
        return pltpu.make_async_copy(x_hbm.at[:, span], xbuf.at[pl.ds(0, rows), span], x_sem.at[k])

    def w_copies(k):
        src, dst = pl.ds(k * CHUNK, CHUNK), pl.ds((k % SLOTS) * CHUNK, CHUNK)
        return (
            pltpu.make_async_copy(wg_hbm.at[src, mine], wgu.at[dst, pl.ds(0, part)], w_sem.at[0, k]),
            pltpu.make_async_copy(wu_hbm.at[src, mine], wgu.at[dst, pl.ds(part, part)], w_sem.at[1, k]),
        )

    offs = [far]
    for d in range(far - 1, 0, -1):
        offs += [d, -d]
    offs.append(0)
    place = {off: i for i, off in enumerate(offs)}
    place[-far] = place[far]

    def d_copy(p):
        span = pl.ds(pl.multiple_of(owner(offs[p]) * cols, 128), cols)
        return pltpu.make_async_copy(
            wd_hbm.at[pl.ds(pl.multiple_of(side * part, 128), part), span], wd.at[p], d_sem.at[p]
        )

    for k in range(min(SLOTS, chunks)):
        x_copy(k).start()
        for c in w_copies(k):
            c.start()
    for k in range(SLOTS, chunks):
        x_copy(k).start()

    pl.semaphore_wait(barrier, 3)

    def x_send(k):
        span = pl.ds(k * CHUNK, CHUNK)
        return pltpu.make_async_remote_copy(
            x_hbm.at[:, span], xbuf.at[pl.ds(rows, rows), span], xs_sem.at[k], xr_sem.at[k],
            device_id=partner, device_id_type=mesh_id,
        )

    for k in range(chunks):
        x_send(k).start()

    k = 0
    for g, size in enumerate(GROUPS):
        for j in range(k, k + size):
            x_copy(j).wait()
            x_send(j).wait_recv()
            for c in w_copies(j):
                c.wait()
        span = pl.ds(k * CHUNK, size * CHUNK)
        slot = pl.ds((k % SLOTS) * CHUNK, size * CHUNK)
        if g < len(GROUPS) - 1:
            got = jnp.dot(xbuf[:, span], wgu[slot, :], preferred_element_type=F32)
            acc[...] = got if g == 0 else acc[...] + got
        else:
            at = 0
            while at < part:
                width = min(256, part - at)
                gs, us = pl.ds(at, width), pl.ds(part + at, width)
                gate = acc[:, gs] + jnp.dot(xbuf[:, span], wgu[slot, gs], preferred_element_type=F32)
                up = acc[:, us] + jnp.dot(xbuf[:, span], wgu[slot, us], preferred_element_type=F32)
                hid[:, gs] = (jax.nn.silu(gate) * up).astype(BF16)
                at += width
        for j in range(k, k + size):
            if j + SLOTS < chunks:
                for c in w_copies(j + SLOTS):
                    c.start()
            if j + SLOTS == chunks - 1:
                for p in range(n):
                    d_copy(p).start()
        k += size

    def p_send(p):
        return pltpu.make_async_remote_copy(
            psend.at[p], precv.at[p], ps_sem.at[p], pr_sem.at[p], device_id=partner, device_id_type=mesh_id
        )

    def down(p):
        d_copy(p).wait()
        got = jnp.dot(hid[...], wd[p], preferred_element_type=F32)
        psend[p] = got[rows:].astype(BF16)
        p_send(p).start()
        term[p] = got[:rows]

    joined = set()

    def join(p):
        if p not in joined:
            joined.add(p)
            p_send(p).wait_recv()

    def piece(h, u):
        return pl.ds(h * half_rows + u * sub_rows, sub_rows)

    def rs_step(way, t):
        h = (way + t) % 2
        return h, far - (t + 1) // 2

    def ag_step(way, t):
        return (way + t) % 2, t // 2

    hops = n - 1

    def rs_send(way, t, u):
        part_rows = pl.ds(u * sub_rows, sub_rows)
        return pltpu.make_async_remote_copy(
            rsend.at[way, t, part_rows], rrecv.at[way, t, part_rows], s_sem.at[way, t, u], r_sem.at[way, t, u],
            device_id=to[way], device_id_type=mesh_id,
        )

    def ag_ref(way, t, u, received):
        h, e = ag_step(way, t)
        e += received
        return y.at[owner(-e if way == 0 else e), piece(h, u)]

    def ag_send(way, t, u):
        ref = ag_ref(way, t, u, 0)
        return pltpu.make_async_remote_copy(
            ref, ref, s_sem.at[way, hops + t, u], r_sem.at[way, hops + t, u], device_id=to[way], device_id_type=mesh_id
        )

    def own(p, h, u):
        return term[p, piece(h, u)] + precv[p, piece(h, u)].astype(F32)

    def rs_slot(t):
        for u in range(SUBS):
            for way in range(2):
                h, d = rs_step(way, t)
                p = place[d if way == 0 else -d]
                join(p)
                total = own(p, h, u)
                if t >= 2:
                    rs_send(way, t - 2, u).wait_recv()
                    total = total + rrecv[way, t - 2, pl.ds(u * sub_rows, sub_rows)].astype(F32)
                rsend[way, t, pl.ds(u * sub_rows, sub_rows)] = total.astype(BF16)
                rs_send(way, t, u).start()

    def finish(h, u):
        p = place[0]
        join(p)
        total = own(p, h, u)
        for way in range(2):
            t = hops - 1 if rs_step(way, hops - 1)[0] == h else hops - 2
            rs_send(way, t, u).wait_recv()
            total = total + rrecv[way, t, pl.ds(u * sub_rows, sub_rows)].astype(F32)
        y[me, piece(h, u)] = total.astype(BF16)

    down(0)
    down(1)
    rs_slot(0)
    down(2)
    rs_slot(1)
    nxt = 3
    for t in range(2, hops):
        while nxt < n and (t % 2 == 0):
            down(nxt)
            nxt += 1
            if nxt % 2 == 1 and nxt < n:
                break
        rs_slot(t)
    while nxt < n:
        down(nxt)
        nxt += 1

    def out_copy(c, h):
        span = pl.ds(h * half_rows, half_rows)
        return pltpu.make_async_copy(
            y.at[c, span], y_hbm.at[span, pl.ds(pl.multiple_of(c * cols, 128), cols)], o_sem.at[c, h]
        )

    for u in range(SUBS):
        for way in range(2):
            finish(way, u)
            for w in (way, 1 - way):
                t = [t for t in range(2) if ag_step(w, t)[0] == way][0]
                ag_send(w, t, u).start()
    for h in range(2):
        out_copy(me, h).start()

    for t in range(2, hops + 2):
        for u in range(SUBS):
            for way in range(2):
                ag_send(way, t - 2, u).wait_recv()
                if t < hops:
                    ag_send(way, t, u).start()
        for way in range(2):
            h, e = ag_step(way, t)
            out_copy(owner(-e if way == 0 else e), h).start()

    for off in range(n):
        for h in range(2):
            out_copy(owner(off), h).wait()
    for k in range(chunks):
        x_send(k).wait_send()
    for p in range(n):
        p_send(p).wait_send()
    for way in range(2):
        for t in range(hops):
            for u in range(SUBS):
                rs_send(way, t, u).wait_send()
                ag_send(way, t, u).wait_send()


def solution(mesh):
    n = mesh.shape["tp"]

    def step(x, w_gate, w_up, w_down):
        rows, depth = x.shape
        share = w_gate.shape[1]
        part, cols, chunks = share // 2, depth // n, depth // CHUNK
        hops = n - 1
        dma = pltpu.SemaphoreType.DMA
        return pl.pallas_call(
            functools.partial(kernel, n),
            out_shape=jax.ShapeDtypeStruct((rows, depth), BF16),
            in_specs=[pl.BlockSpec(memory_space=pl.ANY)] * 4,
            out_specs=pl.BlockSpec(memory_space=pl.ANY),
            scratch_shapes=[
                pltpu.VMEM((2 * rows, depth), BF16),
                pltpu.VMEM((SLOTS * CHUNK, share), BF16),
                pltpu.VMEM((n, part, cols), BF16),
                pltpu.VMEM((2 * rows, share), F32),
                pltpu.VMEM((2 * rows, part), BF16),
                pltpu.VMEM((n, rows, cols), F32),
                pltpu.VMEM((n, rows, cols), BF16),
                pltpu.VMEM((n, rows, cols), BF16),
                pltpu.VMEM((2, hops, rows // 2, cols), BF16),
                pltpu.VMEM((2, hops, rows // 2, cols), BF16),
                pltpu.VMEM((n, rows, cols), BF16),
                dma((chunks,)),
                dma((chunks,)),
                dma((chunks,)),
                dma((2, chunks)),
                dma((n,)),
                dma((n,)),
                dma((n,)),
                dma((2, 2 * hops, SUBS)),
                dma((2, 2 * hops, SUBS)),
                dma((n, 2)),
            ],
            compiler_params=pltpu.CompilerParams(
                collective_id=0, has_side_effects=True, vmem_limit_bytes=67043328
            ),
        )(x, w_gate, w_up, w_down)

    return jax.shard_map(
        step,
        mesh=mesh,
        in_specs=(P("dp", None), P(None, "tp"), P(None, "tp"), P("tp", None)),
        out_specs=P("dp", None),
        check_vma=False,
    )
```

time: 134 us -> 69.1 us (0.52)
  waiting for transfers between devices: 77 us -> 0 us
  Pallas kernels: 0 us -> 66.1 us
  matrix products: 38.6 us -> 0 us
  between operations: 13.4 us -> 0.01 us
  local copies, waits for them, and re-layouts: 4.35 us -> 2.85 us
    psum x1 -> x0, waiting for transfers between devices: 77 us -> none  [step(): return lax.psum(term, 'tp')]
    pallas_call x0 -> x1, Pallas kernels: none -> 66.1 us  [step(): pl.pallas_call(functools.partial(kernel, n), out_shape=jax.ShapeDtypeStru...]
    dot_general x2 -> x0, matrix products: 38.6 us -> none  [the longest x1 25.6 us: step(): jnp.dot(hidden, w_down, preferred_element_type=jnp.float32)]
    unnamed x5 -> x1, local copies, waits for them, and re-layouts: 4.35 us -> 2.85 us
  transfers between devices with their start and end apart: 1 -> 0, of which waited for: 1 -> 0; matrix products, arithmetic and copies ran while one was open for 0% -> 0% of each run, Pallas kernels for 0% -> 0%
where the time goes in v1:
time: 69.1 us; the launch traced here: 69 us
  Pallas kernels  66.1 us (96%)
  local copies, waits for them, and re-layouts  2.85 us (4%)
    pallas_call x1, Pallas kernels, step(): pl.pallas_call(functools.partial(kernel, n), out_shape=jax.ShapeDtypeStru...  66.1 us
    unnamed x1, local copies, waits for them, and re-layouts  2.85 us

profile of v1, /device:TPU:30, one launch (start us, length us, event | category | flops | bytes accessed | tf_op | source)
XLA Modules:
  0.0 69.0 jit_solution(9431053315332311676)
XLA Ops:
  0.0 66.1 %shard_map.46 = bf16[128,7168]{1,0:T(8,128)(2,1)} custom-call(bf16[128,7168]{1,0:T(8,128)(2,1)} %x_hbm.1, bf16[7168,2304]{1,0:T(8,128)(2,1)} %wg_hbm.1, bf16[7168,2304]{1,0:T(8,128)(2,1)} %wu_hbm.1, bf16[2304,7168]{1,0:T(8,128)(2,1)} %wd_hbm.1), custom_call_target="tpu_custom_call" | custom-call | tf_op jit(solution)/shard_map/pallas_call | solution.py:257
  66.1 2.8 %copy.6 = bf16[128,7168]{1,0:T(8,128)(2,1)} copy(bf16[128,7168]{1,0:T(8,128)(2,1)} %shard_map.46) | data formatting | bytes 3670016

commit v2 on v0

v2 whole, which is shorter than its diff:
```python
import functools

import jax
import jax.numpy as jnp
from jax import lax
from jax.experimental import pallas as pl
from jax.experimental.pallas import tpu as pltpu
from jax.sharding import PartitionSpec as P

F32, BF16 = jnp.float32, jnp.bfloat16
CHUNK = 1024
SLOTS = 5
SUBS = 4
ACT_ROWS = 32


def kernel(n, x_hbm, wg_hbm, wu_hbm, wd_hbm, y, xbuf, wgu, wd, acc, hid, term, psend, precv, rsend, rrecv,
           x_sem, xs_sem, xr_sem, w_sem, d_sem, ps_sem, pr_sem, s_sem, r_sem):
    rows, depth = x_hbm.shape
    part = wg_hbm.shape[1] // 2
    cols = depth // n
    half_rows = rows // 2
    sub_rows = half_rows // SUBS
    far = n // 2
    hops = n - 1
    chunks = depth // CHUNK

    dp, me = lax.axis_index("dp"), lax.axis_index("tp")
    side = lax.rem(dp, 2)
    partner = {"dp": dp + 1 - 2 * side}
    right, left = {"tp": lax.rem(me + 1, n)}, {"tp": lax.rem(me + n - 1, n)}
    to = (right, left)
    mesh_id = pl.DeviceIdType.MESH

    barrier = pltpu.get_barrier_semaphore()
    for other in (left, right, partner):
        pl.semaphore_signal(barrier, inc=1, device_id=other, device_id_type=mesh_id)

    def owner(off):
        return lax.rem(me + off + n, n)

    mine = pl.ds(pl.multiple_of(side * part, 128), part)

    def span(k):
        return pl.ds(pl.multiple_of(k * CHUNK, CHUNK), CHUNK)

    def x_copy(k):
        return pltpu.make_async_copy(x_hbm.at[:, span(k)], xbuf.at[k, pl.ds(0, rows)], x_sem.at[k])

    def w_copies(k):
        slot = lax.rem(k, SLOTS)
        return (
            pltpu.make_async_copy(wg_hbm.at[span(k), mine], wgu.at[slot, :, pl.ds(0, part)], w_sem.at[0, k]),
            pltpu.make_async_copy(wu_hbm.at[span(k), mine], wgu.at[slot, :, pl.ds(part, part)], w_sem.at[1, k]),
        )

    def at(p):
        dist = far - (p + 1) // 2
        return owner(dist * (2 * lax.rem(p, 2) - 1))

    def d_copy(p):
        return pltpu.make_async_copy(
            wd_hbm.at[mine, pl.ds(pl.multiple_of(at(p) * cols, 128), cols)], wd.at[p], d_sem.at[p]
        )

    def start_all(*copies):
        for c in copies:
            c.start()

    def x_send(k):
        return pltpu.make_async_remote_copy(
            x_hbm.at[:, span(k)], xbuf.at[k, pl.ds(rows, rows)], xs_sem.at[k], xr_sem.at[k],
            device_id=partner, device_id_type=mesh_id,
        )

    def loop(lo, hi, body):
        def run(i, carry):
            body(i)
            return carry

        lax.fori_loop(lo, hi, run, 0)

    loop(0, SLOTS, lambda k: start_all(x_copy(k), *w_copies(k)))
    loop(SLOTS, chunks, lambda k: start_all(x_copy(k)))
    pl.semaphore_wait(barrier, 3)
    loop(0, chunks, lambda k: start_all(x_send(k)))

    def zero(r):
        acc[pl.ds(pl.multiple_of(r * 16, 16), 16)] = jnp.zeros((16, 2 * part), F32)

    loop(0, 2 * rows // 16, zero)

    def gate_up(k):
        for c in w_copies(k):
            c.wait()
        x_copy(k).wait()
        x_send(k).wait_recv()
        acc[...] += jnp.dot(xbuf[k], wgu[lax.rem(k, SLOTS)], preferred_element_type=F32)

        @pl.when(k + SLOTS < chunks)
        def _():
            start_all(*w_copies(k + SLOTS))

        @pl.when(k + SLOTS == chunks - 1)
        def _():
            loop(0, n, lambda p: start_all(d_copy(p)))

    loop(0, chunks, gate_up)

    def activate(r):
        here = pl.ds(pl.multiple_of(r * ACT_ROWS, ACT_ROWS), ACT_ROWS)
        hid[here] = (jax.nn.silu(acc[here, :part]) * acc[here, part:]).astype(BF16)

    loop(0, 2 * rows // ACT_ROWS, activate)

    def p_send(p):
        return pltpu.make_async_remote_copy(
            psend.at[p], precv.at[p], ps_sem.at[p], pr_sem.at[p], device_id=partner, device_id_type=mesh_id
        )

    def down(p):
        d_copy(p).wait()
        got = jnp.dot(hid[...], wd[p], preferred_element_type=F32)
        psend[p] = got[rows:].astype(BF16)
        p_send(p).start()
        term[p] = got[:rows]

    def piece(h, u):
        return pl.ds(pl.multiple_of(h * half_rows + u * sub_rows, sub_rows), sub_rows)

    def sub(u):
        return pl.ds(pl.multiple_of(u * sub_rows, sub_rows), sub_rows)

    def half(way, t):
        return lax.rem(way + t, 2)

    def rs_send(way, t, u):
        return pltpu.make_async_remote_copy(
            rsend.at[way, t, sub(u)], rrecv.at[way, t, sub(u)], s_sem.at[way, t, u], r_sem.at[way, t, u],
            device_id=to[way], device_id_type=mesh_id,
        )

    def ag_send(way, t, u):
        c = owner(-(t // 2) if way == 0 else t // 2)
        ref = y.at[piece(half(way, t), u), pl.ds(pl.multiple_of(c * cols, 128), cols)]
        return pltpu.make_async_remote_copy(
            ref, ref, s_sem.at[way, hops + t, u], r_sem.at[way, hops + t, u], device_id=to[way], device_id_type=mesh_id
        )

    def own(p, h, u):
        return term[p, piece(h, u)] + precv[p, piece(h, u)].astype(F32)

    def rs_place(way, t):
        first = 1 - (t + hops - 1) // hops
        p = 2 * ((t + 1) // 2)
        return p if way else p - 1 + first

    def rs_slot(t):
        @pl.when(t == 0)
        def _():
            p_send(0).wait_recv()

        @pl.when(lax.rem(t, 2) == 1)
        def _():
            p_send(t).wait_recv()
            p_send(t + 1).wait_recv()

        @pl.when(t < 2)
        def _():
            def begin(u):
                for way in range(2):
                    rsend[way, t, sub(u)] = own(rs_place(way, t), half(way, t), u).astype(BF16)
                    rs_send(way, t, u).start()

            loop(0, SUBS, begin)

        @pl.when(t >= 2)
        def _():
            def go_on(u):
                for way in range(2):
                    total = own(rs_place(way, t), half(way, t), u)
                    rs_send(way, t - 2, u).wait_recv()
                    total = total + rrecv[way, t - 2, sub(u)].astype(F32)
                    rsend[way, t, sub(u)] = total.astype(BF16)
                    rs_send(way, t, u).start()

            loop(0, SUBS, go_on)

    def down_and_ring(p):
        down(p)

        @pl.when(p >= 1)
        def _():
            rs_slot(p - 1)

    loop(0, n, down_and_ring)
    p_send(hops).wait_recv()

    mine_y = pl.ds(pl.multiple_of(me * cols, 128), cols)

    def finish(u):
        for h in range(2):
            total = own(hops, h, u)
            for way in range(2):
                t = hops - 1 if (way + hops - 1) % 2 == h else hops - 2
                rs_send(way, t, u).wait_recv()
                total = total + rrecv[way, t, sub(u)].astype(F32)
            y[piece(h, u), mine_y] = total.astype(BF16)
            for way in (h, 1 - h):
                ag_send(way, (h + way) % 2, u).start()

    loop(0, SUBS, finish)

    def forward(t):
        def one(u):
            for way in range(2):
                ag_send(way, t - 2, u).wait_recv()
                ag_send(way, t, u).start()

        loop(0, SUBS, one)

    loop(2, hops, forward)

    def last(u):
        for t in (hops - 2, hops - 1):
            for way in range(2):
                ag_send(way, t, u).wait_recv()

    loop(0, SUBS, last)

    loop(0, chunks, lambda k: x_send(k).wait_send())
    loop(0, n, lambda p: p_send(p).wait_send())

    def sent(t):
        def one(u):
            for way in range(2):
                rs_send(way, t, u).wait_send()
                ag_send(way, t, u).wait_send()

        loop(0, SUBS, one)

    loop(0, hops, sent)


def solution(mesh):
    n = mesh.shape["tp"]

    def step(x, w_gate, w_up, w_down):
        rows, depth = x.shape
        share = w_gate.shape[1]
        part, cols, chunks = share // 2, depth // n, depth // CHUNK
        hops = n - 1
        dma = pltpu.SemaphoreType.DMA
        return pl.pallas_call(
            functools.partial(kernel, n),
            out_shape=pltpu.VMEM((rows, depth), BF16),
            in_specs=[pl.BlockSpec(memory_space=pl.ANY)] * 4,
            out_specs=pl.BlockSpec(memory_space=pltpu.VMEM),
            scratch_shapes=[
                pltpu.VMEM((chunks, 2 * rows, CHUNK), BF16),
                pltpu.VMEM((SLOTS, CHUNK, share), BF16),
                pltpu.VMEM((n, part, cols), BF16),
                pltpu.VMEM((2 * rows, share), F32),
                pltpu.VMEM((2 * rows, part), BF16),
                pltpu.VMEM((n, rows, cols), F32),
                pltpu.VMEM((n, rows, cols), BF16),
                pltpu.VMEM((n, rows, cols), BF16),
                pltpu.VMEM((2, hops, rows // 2, cols), BF16),
                pltpu.VMEM((2, hops, rows // 2, cols), BF16),
                dma((chunks,)),
                dma((chunks,)),
                dma((chunks,)),
                dma((2, chunks)),
                dma((n,)),
                dma((n,)),
                dma((n,)),
                dma((2, 2 * hops, SUBS)),
                dma((2, 2 * hops, SUBS)),
            ],
            compiler_params=pltpu.CompilerParams(
                collective_id=0, has_side_effects=True, vmem_limit_bytes=62 * 1024 * 1024
            ),
        )(x, w_gate, w_up, w_down)

    return jax.shard_map(
        step,
        mesh=mesh,
        in_specs=(P("dp", None), P(None, "tp"), P(None, "tp"), P("tp", None)),
        out_specs=P("dp", None),
        check_vma=False,
    )
```

time: 134 us -> 62.6 us (0.47)
  waiting for transfers between devices: 77 us -> 0 us
  Pallas kernels: 0 us -> 61.3 us
  matrix products: 38.6 us -> 0 us
  between operations: 13.4 us -> 0.01 us
  local copies, waits for them, and re-layouts: 4.35 us -> 1.23 us
    psum x1 -> x0, waiting for transfers between devices: 77 us -> none  [step(): return lax.psum(term, 'tp')]
    pallas_call x0 -> x1, Pallas kernels: none -> 61.3 us  [step(): pl.pallas_call(functools.partial(kernel, n), out_shape=pltpu.VMEM((rows,...]
    dot_general x2 -> x0, matrix products: 38.6 us -> none  [the longest x1 25.6 us: step(): jnp.dot(hidden, w_down, preferred_element_type=jnp.float32)]
    unnamed x5 -> x1, local copies, waits for them, and re-layouts: 4.35 us -> 1.23 us
  transfers between devices with their start and end apart: 1 -> 0, of which waited for: 1 -> 0; matrix products, arithmetic and copies ran while one was open for 0% -> 0% of each run, Pallas kernels for 0% -> 0%
where the time goes in v2:
time: 62.6 us; the launch traced here: 62.5 us
  Pallas kernels  61.3 us (98%)
  local copies, waits for them, and re-layouts  1.23 us (2%)
    pallas_call x1, Pallas kernels, step(): pl.pallas_call(functools.partial(kernel, n), out_shape=pltpu.VMEM((rows,...  61.3 us

profile of v2, /device:TPU:30, one launch (start us, length us, event | category | flops | bytes accessed | tf_op | source)
XLA Modules:
  0.0 62.5 jit_solution(5717512124308455987)
XLA Ops:
  0.0 61.3 %shard_map.46 = bf16[128,7168]{1,0:T(8,128)(2,1)S(1)} custom-call(bf16[128,7168]{1,0:T(8,128)(2,1)} %x_hbm.1, bf16[7168,2304]{1,0:T(8,128)(2,1)} %wg_hbm.1, bf16[7168,2304]{1,0:T(8,128)(2,1)} %wu_hbm.1, bf16[2304,7168]{1,0:T(8,128)(2,1)} %wd_hbm.1), custom_call_target="tpu_custom_call" | custom-call | tf_op jit(solution)/shard_map/pallas_call | solution.py:254
  61.3 1.2 %copy.6 = bf16[128,7168]{1,0:T(8,128)(2,1)} copy(bf16[128,7168]{1,0:T(8,128)(2,1)S(1)} %shard_map.46) | data formatting | bytes 3670016

commit v3 on v2

v3 whole, which is shorter than its diff:
```python
import functools

import jax
import jax.numpy as jnp
from jax import lax
from jax.experimental import pallas as pl
from jax.experimental.pallas import tpu as pltpu
from jax.sharding import PartitionSpec as P

F32, BF16 = jnp.float32, jnp.bfloat16
CHUNK = 1024
SLOTS = 5
FINE = 4
COARSE = 2
ACT_ROWS = 32


def kernel(n, x_hbm, wg_hbm, wu_hbm, wd_hbm, y, xbuf, wgu, wd, acc, hid, term, psend, precv, rsend, rrecv,
           x_sem, xs_sem, xr_sem, w_sem, d_sem, ps_sem, pr_sem, s_sem, fine_sem, coarse_sem):
    rows, depth = x_hbm.shape
    part = wg_hbm.shape[1] // 2
    cols = depth // n
    half_rows = rows // 2
    far = n // 2
    hops = n - 1
    chunks = depth // CHUNK

    dp, me = lax.axis_index("dp"), lax.axis_index("tp")
    side = lax.rem(dp, 2)
    partner = {"dp": dp + 1 - 2 * side}
    right, left = {"tp": lax.rem(me + 1, n)}, {"tp": lax.rem(me + n - 1, n)}
    to = (right, left)
    mesh_id = pl.DeviceIdType.MESH

    barrier = pltpu.get_barrier_semaphore()
    for other in (left, right, partner):
        pl.semaphore_signal(barrier, inc=1, device_id=other, device_id_type=mesh_id)

    def owner(off):
        return lax.rem(me + off + n, n)

    mine = pl.ds(pl.multiple_of(side * part, 128), part)

    def span(k):
        return pl.ds(pl.multiple_of(k * CHUNK, CHUNK), CHUNK)

    x_copy = pltpu.make_async_copy(x_hbm, xbuf.at[pl.ds(0, rows)], x_sem)

    def w_copies(k):
        slot = lax.rem(k, SLOTS)
        return (
            pltpu.make_async_copy(wg_hbm.at[span(k), mine], wgu.at[slot, :, pl.ds(0, part)], w_sem.at[k]),
            pltpu.make_async_copy(wu_hbm.at[span(k), mine], wgu.at[slot, :, pl.ds(part, part)], w_sem.at[k]),
        )

    def w_wait(k):
        pltpu.make_async_copy(wg_hbm.at[span(k)], wgu.at[lax.rem(k, SLOTS)], w_sem.at[k]).wait()

    def at(p):
        dist = far - (p + 1) // 2
        return owner(dist * (2 * lax.rem(p, 2) - 1))

    def d_copy(p):
        return pltpu.make_async_copy(
            wd_hbm.at[mine, pl.ds(pl.multiple_of(at(p) * cols, 128), cols)], wd.at[p], d_sem.at[p]
        )

    def start_all(*copies):
        for c in copies:
            c.start(priority=1)

    def x_send(k):
        return pltpu.make_async_remote_copy(
            xbuf.at[pl.ds(0, rows), span(k)], xbuf.at[pl.ds(rows, rows), span(k)], xs_sem, xr_sem.at[k],
            device_id=partner, device_id_type=mesh_id,
        )

    def loop(lo, hi, body):
        def run(i, carry):
            body(i)
            return carry

        lax.fori_loop(lo, hi, run, 0)

    x_copy.start()
    loop(0, SLOTS, lambda k: start_all(*w_copies(k)))
    pl.semaphore_wait(barrier, 3)

    x_copy.wait()
    loop(0, chunks, lambda k: x_send(k).start())

    def zero(r):
        acc[pl.ds(pl.multiple_of(r * 16, 16), 16)] = jnp.zeros((16, 2 * part), F32)

    loop(0, 2 * rows // 16, zero)

    def gate_up(k):
        w_wait(k)
        x_send(k).wait_recv()
        acc[...] += jnp.dot(xbuf[:, span(k)], wgu[lax.rem(k, SLOTS)], preferred_element_type=F32)

        @pl.when(k + SLOTS < chunks)
        def _():
            start_all(*w_copies(k + SLOTS))

        @pl.when(k + SLOTS == chunks - 1)
        def _():
            loop(0, n, lambda p: start_all(d_copy(p)))

    loop(0, chunks, gate_up)

    def activate(r):
        here = pl.ds(pl.multiple_of(r * ACT_ROWS, ACT_ROWS), ACT_ROWS)
        hid[here] = (jax.nn.silu(acc[here, :part]) * acc[here, part:]).astype(BF16)

    loop(0, 2 * rows // ACT_ROWS, activate)

    def p_send(p):
        return pltpu.make_async_remote_copy(
            psend.at[p], precv.at[p], ps_sem, pr_sem.at[p], device_id=partner, device_id_type=mesh_id
        )

    def down(p):
        d_copy(p).wait()
        got = jnp.dot(hid[...], wd[p], preferred_element_type=F32)
        psend[p] = got[rows:].astype(BF16)
        p_send(p).start()
        term[p] = got[:rows]

    def half(way, t):
        return lax.rem(way + t, 2)

    def span_of(h, u, count):
        size = half_rows // count
        return pl.ds(pl.multiple_of(h * half_rows + u * size, size), size)

    def r_sem(way, slot, u, count):
        if count == FINE:
            return fine_sem.at[way, slot - (hops - 2), u]
        return coarse_sem.at[way, slot - 4 * (slot // (hops + 2)), u]

    def rs_send(way, t, u, count):
        here = span_of(0, u, count)
        return pltpu.make_async_remote_copy(
            rsend.at[way, t, here], rrecv.at[way, t, here], s_sem.at[0, way], r_sem(way, t, u, count),
            device_id=to[way], device_id_type=mesh_id,
        )

    def ag_send(way, t, u, count):
        c = owner(-(t // 2) if way == 0 else t // 2)
        ref = y.at[span_of(half(way, t), u, count), pl.ds(pl.multiple_of(c * cols, 128), cols)]
        return pltpu.make_async_remote_copy(
            ref, ref, s_sem.at[1, way], r_sem(way, hops + t, u, count), device_id=to[way], device_id_type=mesh_id
        )

    def own(p, h, u, count):
        here = span_of(h, u, count)
        return term[p, here] + precv[p, here].astype(F32)

    def rs_place(way, t):
        first = 1 - (t + hops - 1) // hops
        p = 2 * ((t + 1) // 2)
        return p if way else p - 1 + first

    def rs_slot(t):
        @pl.when(t == 0)
        def _():
            p_send(0).wait_recv()

        @pl.when(lax.rem(t, 2) == 1)
        def _():
            p_send(t).wait_recv()
            p_send(t + 1).wait_recv()

        def pass_on(way, u, count, add):
            total = own(rs_place(way, t), half(way, t), u, count)
            here = span_of(0, u, count)
            if add:
                total = total + rrecv[way, t - 2, here].astype(F32)
            rsend[way, t, here] = total.astype(BF16)
            rs_send(way, t, u, count).start()

        @pl.when(t < 2)
        def _():
            def begin(u):
                for way in range(2):
                    pass_on(way, u, COARSE, False)

            loop(0, COARSE, begin)

        @pl.when((t >= 2) & (t < hops - 2))
        def _():
            def middle(u):
                for way in range(2):
                    rs_send(way, t - 2, u, COARSE).wait_recv()
                    pass_on(way, u, COARSE, True)

            loop(0, COARSE, middle)

        @pl.when(t >= hops - 2)
        def _():
            def end(u):
                for way in range(2):
                    rs_send(way, t - 2, u, COARSE).wait_recv()
                    for v in range(FINE // COARSE):
                        pass_on(way, u * (FINE // COARSE) + v, FINE, True)

            loop(0, COARSE, end)

    def down_and_ring(p):
        down(p)

        @pl.when(p >= 1)
        def _():
            rs_slot(p - 1)

    loop(0, n, down_and_ring)
    p_send(hops).wait_recv()

    mine_y = pl.ds(pl.multiple_of(me * cols, 128), cols)

    def finish(u):
        for h in range(2):
            total = own(hops, h, u, FINE)
            for way in range(2):
                t = hops - 1 if (way + hops - 1) % 2 == h else hops - 2
                rs_send(way, t, u, FINE).wait_recv()
                total = total + rrecv[way, t, span_of(0, u, FINE)].astype(F32)
            y[span_of(h, u, FINE), mine_y] = total.astype(BF16)
            for way in (h, 1 - h):
                ag_send(way, (h + way) % 2, u, FINE).start()

    loop(0, FINE, finish)

    def forward_first(t):
        def one(u):
            for way in range(2):
                for v in range(FINE // COARSE):
                    ag_send(way, t - 2, u * (FINE // COARSE) + v, FINE).wait_recv()
                ag_send(way, t, u, COARSE).start()

        loop(0, COARSE, one)

    def forward(t):
        def one(u):
            for way in range(2):
                ag_send(way, t - 2, u, COARSE).wait_recv()
                ag_send(way, t, u, COARSE).start()

        loop(0, COARSE, one)

    loop(2, 4, forward_first)
    loop(4, hops, forward)

    def last(u):
        for t in (hops - 2, hops - 1):
            for way in range(2):
                ag_send(way, t, u, COARSE).wait_recv()

    loop(0, COARSE, last)

    pltpu.make_async_remote_copy(
        xbuf.at[pl.ds(0, rows)], xbuf.at[pl.ds(rows, rows)], xs_sem, xr_sem.at[0], device_id=partner, device_id_type=mesh_id
    ).wait_send()
    pltpu.make_async_remote_copy(
        psend, precv, ps_sem, pr_sem.at[0], device_id=partner, device_id_type=mesh_id
    ).wait_send()
    for way in range(2):
        for stage in range(2):
            pltpu.make_async_remote_copy(
                rsend.at[way], rrecv.at[way], s_sem.at[stage, way], coarse_sem.at[0, 0, 0],
                device_id=to[way], device_id_type=mesh_id,
            ).wait_send()


def solution(mesh):
    n = mesh.shape["tp"]

    def step(x, w_gate, w_up, w_down):
        rows, depth = x.shape
        share = w_gate.shape[1]
        part, cols, chunks = share // 2, depth // n, depth // CHUNK
        hops = n - 1
        dma = pltpu.SemaphoreType.DMA
        return pl.pallas_call(
            functools.partial(kernel, n),
            out_shape=pltpu.VMEM((rows, depth), BF16),
            in_specs=[pl.BlockSpec(memory_space=pl.ANY)] * 4,
            out_specs=pl.BlockSpec(memory_space=pltpu.VMEM),
            scratch_shapes=[
                pltpu.VMEM((2 * rows, depth), BF16),
                pltpu.VMEM((SLOTS, CHUNK, share), BF16),
                pltpu.VMEM((n, part, cols), BF16),
                pltpu.VMEM((2 * rows, share), F32),
                pltpu.VMEM((2 * rows, part), BF16),
                pltpu.VMEM((n, rows, cols), F32),
                pltpu.VMEM((n, rows, cols), BF16),
                pltpu.VMEM((n, rows, cols), BF16),
                pltpu.VMEM((2, hops, rows // 2, cols), BF16),
                pltpu.VMEM((2, hops, rows // 2, cols), BF16),
                dma,
                dma,
                dma((chunks,)),
                dma((chunks,)),
                dma((n,)),
                dma,
                dma((n,)),
                dma((2, 2)),
                dma((2, 4, FINE)),
                dma((2, 2 * (hops - 2), COARSE)),
            ],
            compiler_params=pltpu.CompilerParams(
                collective_id=0, has_side_effects=True, vmem_limit_bytes=62 * 1024 * 1024
            ),
        )(x, w_gate, w_up, w_down)

    return jax.shard_map(
        step,
        mesh=mesh,
        in_specs=(P("dp", None), P(None, "tp"), P(None, "tp"), P("tp", None)),
        out_specs=P("dp", None),
        check_vma=False,
    )
```

time: 62.6 us -> 60.7 us (0.970)
  Pallas kernels: 61.3 us -> 59.4 us
    pallas_call x1, Pallas kernels: 61.3 us -> 59.4 us  [step(): pl.pallas_call(functools.partial(kernel, n), out_shape=pltpu.VMEM((rows,...]
where the time goes in v3:
time: 60.7 us
  Pallas kernels  59.4 us (98%)
  local copies, waits for them, and re-layouts  1.23 us (2%)
    pallas_call x1, Pallas kernels, step(): pl.pallas_call(functools.partial(kernel, n), out_shape=pltpu.VMEM((rows,...  59.4 us
    unnamed x1, local copies, waits for them, and re-layouts  1.23 us

profile of v3, /device:TPU:30, one launch (start us, length us, event | category | flops | bytes accessed | tf_op | source)
XLA Modules:
  0.0 60.7 jit_solution(17248704417990782108)
XLA Ops:
  0.0 59.4 %shard_map.46 = bf16[128,7168]{1,0:T(8,128)(2,1)S(1)} custom-call(bf16[128,7168]{1,0:T(8,128)(2,1)} %x_hbm.1, bf16[7168,2304]{1,0:T(8,128)(2,1)} %wg_hbm.1, bf16[7168,2304]{1,0:T(8,128)(2,1)} %wu_hbm.1, bf16[2304,7168]{1,0:T(8,128)(2,1)} %wd_hbm.1), custom_call_target="tpu_custom_call" | custom-call | tf_op jit(solution)/shard_map/pallas_call | solution.py:285
  59.4 1.2 %copy.6 = bf16[128,7168]{1,0:T(8,128)(2,1)} copy(bf16[128,7168]{1,0:T(8,128)(2,1)S(1)} %shard_map.46) | data formatting | bytes 3670016

commit v4 on v3

--- a/solution.py
+++ b/solution.py
@@ -32,10 +32,6 @@
     to = (right, left)
     mesh_id = pl.DeviceIdType.MESH
 
-    barrier = pltpu.get_barrier_semaphore()
-    for other in (left, right, partner):
-        pl.semaphore_signal(barrier, inc=1, device_id=other, device_id_type=mesh_id)
-
     def owner(off):
         return lax.rem(me + off + n, n)
 
@@ -84,6 +80,10 @@
 
     x_copy.start()
     loop(0, SLOTS, lambda k: start_all(*w_copies(k)))
+
+    barrier = pltpu.get_barrier_semaphore()
+    for other in (left, right, partner):
+        pl.semaphore_signal(barrier, inc=1, device_id=other, device_id_type=mesh_id)
     pl.semaphore_wait(barrier, 3)
 
     x_copy.wait()
@@ -208,13 +208,17 @@
             loop(0, COARSE, end)
 
     def down_and_ring(p):
-        down(p)
-
-        @pl.when(p >= 1)
-        def _():
-            rs_slot(p - 1)
-
-    loop(0, n, down_and_ring)
+        @pl.when(p < n)
+        def _():
+            down(p)
+
+        late = p // 6
+
+        @pl.when(lax.rem(p, 2) + late >= 1)
+        def _():
+            rs_slot((1 - late) * ((p - 1) // 2) + late * (p - 3))
+
+    loop(0, hops + 3, down_and_ring)
     p_send(hops).wait_recv()
 
     mine_y = pl.ds(pl.multiple_of(me * cols, 128), cols)

time: 60.7 us -> 60.4 us (level)
  no operation moved by 1% of the time
where the time goes in v4:
time: 60.4 us
  Pallas kernels  59.1 us (98%)
  local copies, waits for them, and re-layouts  1.23 us (2%)
    pallas_call x1, Pallas kernels, step(): pl.pallas_call(functools.partial(kernel, n), out_shape=pltpu.VMEM((rows,...  59.1 us
    unnamed x1, local copies, waits for them, and re-layouts  1.23 us

profile of v4, /device:TPU:30, one launch (start us, length us, event | category | flops | bytes accessed | tf_op | source)
XLA Modules:
  0.0 60.4 jit_solution(3327108514337168688)
XLA Ops:
  0.0 59.1 %shard_map.46 = bf16[128,7168]{1,0:T(8,128)(2,1)S(1)} custom-call(bf16[128,7168]{1,0:T(8,128)(2,1)} %x_hbm.1, bf16[7168,2304]{1,0:T(8,128)(2,1)} %wg_hbm.1, bf16[7168,2304]{1,0:T(8,128)(2,1)} %wu_hbm.1, bf16[2304,7168]{1,0:T(8,128)(2,1)} %wd_hbm.1), custom_call_target="tpu_custom_call" | custom-call | tf_op jit(solution)/shard_map/pallas_call | solution.py:289
  59.1 1.2 %copy.6 = bf16[128,7168]{1,0:T(8,128)(2,1)} copy(bf16[128,7168]{1,0:T(8,128)(2,1)S(1)} %shard_map.46) | data formatting | bytes 3670016

commit v5 on v4

--- a/solution.py
+++ b/solution.py
@@ -137,7 +137,7 @@
     def r_sem(way, slot, u, count):
         if count == FINE:
             return fine_sem.at[way, slot - (hops - 2), u]
-        return coarse_sem.at[way, slot - 4 * (slot // (hops + 2)), u]
+        return coarse_sem.at[way, slot - (hops + 2) * (slot // (hops + 2)), u]
 
     def rs_send(way, t, u, count):
         here = span_of(0, u, count)
@@ -311,7 +311,7 @@
                 dma((n,)),
                 dma((2, 2)),
                 dma((2, 4, FINE)),
-                dma((2, 2 * (hops - 2), COARSE)),
+                dma((2, hops - 2, COARSE)),
             ],
             compiler_params=pltpu.CompilerParams(
                 collective_id=0, has_side_effects=True, vmem_limit_bytes=62 * 1024 * 1024

time: 60.4 us -> 60.3 us (level)
  no operation moved by 1% of the time
where the time goes in v5:
time: 60.3 us; the launch traced here: 60.2 us
  Pallas kernels  59 us (98%)
  local copies, waits for them, and re-layouts  1.23 us (2%)
    pallas_call x1, Pallas kernels, step(): pl.pallas_call(functools.partial(kernel, n), out_shape=pltpu.VMEM((rows,...  59 us
    unnamed x1, local copies, waits for them, and re-layouts  1.23 us

profile of v5, /device:TPU:30, one launch (start us, length us, event | category | flops | bytes accessed | tf_op | source)
XLA Modules:
  0.0 60.2 jit_solution(3779952525060271436)
XLA Ops:
  0.0 59.0 %shard_map.46 = bf16[128,7168]{1,0:T(8,128)(2,1)S(1)} custom-call(bf16[128,7168]{1,0:T(8,128)(2,1)} %x_hbm.1, bf16[7168,2304]{1,0:T(8,128)(2,1)} %wg_hbm.1, bf16[7168,2304]{1,0:T(8,128)(2,1)} %wu_hbm.1, bf16[2304,7168]{1,0:T(8,128)(2,1)} %wd_hbm.1), custom_call_target="tpu_custom_call" | custom-call | tf_op jit(solution)/shard_map/pallas_call | solution.py:289
  59.0 1.2 %copy.6 = bf16[128,7168]{1,0:T(8,128)(2,1)} copy(bf16[128,7168]{1,0:T(8,128)(2,1)S(1)} %shard_map.46) | data formatting | bytes 3670016

commit v6 on v5

--- a/solution.py
+++ b/solution.py
@@ -45,12 +45,12 @@
     def w_copies(k):
         slot = lax.rem(k, SLOTS)
         return (
-            pltpu.make_async_copy(wg_hbm.at[span(k), mine], wgu.at[slot, :, pl.ds(0, part)], w_sem.at[k]),
-            pltpu.make_async_copy(wu_hbm.at[span(k), mine], wgu.at[slot, :, pl.ds(part, part)], w_sem.at[k]),
+            pltpu.make_async_copy(wg_hbm.at[span(k), mine], wgu.at[slot, :, pl.ds(0, part)], w_sem.at[slot]),
+            pltpu.make_async_copy(wu_hbm.at[span(k), mine], wgu.at[slot, :, pl.ds(part, part)], w_sem.at[slot]),
         )
 
     def w_wait(k):
-        pltpu.make_async_copy(wg_hbm.at[span(k)], wgu.at[lax.rem(k, SLOTS)], w_sem.at[k]).wait()
+        pltpu.make_async_copy(wg_hbm.at[span(k)], wgu.at[lax.rem(k, SLOTS)], w_sem.at[lax.rem(k, SLOTS)]).wait()
 
     def at(p):
         dist = far - (p + 1) // 2
@@ -117,7 +117,7 @@
 
     def p_send(p):
         return pltpu.make_async_remote_copy(
-            psend.at[p], precv.at[p], ps_sem, pr_sem.at[p], device_id=partner, device_id_type=mesh_id
+            psend.at[p], precv.at[p], ps_sem, pr_sem.at[(p + 1) // 2], device_id=partner, device_id_type=mesh_id
         )
 
     def down(p):
@@ -169,8 +169,10 @@
 
         @pl.when(lax.rem(t, 2) == 1)
         def _():
-            p_send(t).wait_recv()
-            p_send(t + 1).wait_recv()
+            both = pl.ds(t, 2)
+            pltpu.make_async_remote_copy(
+                psend.at[both], precv.at[both], ps_sem, pr_sem.at[(t + 1) // 2], device_id=partner, device_id_type=mesh_id
+            ).wait_recv()
 
         def pass_on(way, u, count, add):
             total = own(rs_place(way, t), half(way, t), u, count)
@@ -305,10 +307,10 @@
                 dma,
                 dma,
                 dma((chunks,)),
-                dma((chunks,)),
+                dma((SLOTS,)),
                 dma((n,)),
                 dma,
-                dma((n,)),
+                dma((n // 2 + 1,)),
                 dma((2, 2)),
                 dma((2, 4, FINE)),
                 dma((2, hops - 2, COARSE)),

time: 60.3 us -> 60.2 us (level)
  no operation moved by 1% of the time
where the time goes in v6:
time: 60.2 us; the launch traced here: 60.1 us
  Pallas kernels  58.9 us (98%)
  local copies, waits for them, and re-layouts  1.23 us (2%)
    pallas_call x1, Pallas kernels, step(): pl.pallas_call(functools.partial(kernel, n), out_shape=pltpu.VMEM((rows,...  58.9 us
    unnamed x1, local copies, waits for them, and re-layouts  1.23 us

profile of v6, /device:TPU:30, one launch (start us, length us, event | category | flops | bytes accessed | tf_op | source)
XLA Modules:
  0.0 60.1 jit_solution(15007896608870023309)
XLA Ops:
  0.0 58.9 %shard_map.46 = bf16[128,7168]{1,0:T(8,128)(2,1)S(1)} custom-call(bf16[128,7168]{1,0:T(8,128)(2,1)} %x_hbm.1, bf16[7168,2304]{1,0:T(8,128)(2,1)} %wg_hbm.1, bf16[7168,2304]{1,0:T(8,128)(2,1)} %wu_hbm.1, bf16[2304,7168]{1,0:T(8,128)(2,1)} %wd_hbm.1), custom_call_target="tpu_custom_call" | custom-call | tf_op jit(solution)/shard_map/pallas_call | solution.py:291
  58.9 1.2 %copy.6 = bf16[128,7168]{1,0:T(8,128)(2,1)} copy(bf16[128,7168]{1,0:T(8,128)(2,1)S(1)} %shard_map.46) | data formatting | bytes 3670016
